TPU v7x, 32 devices: a whole 2x2x4 slice. The times are simulated.
32 devices in a mesh: pop: 8 (over y, x, core), row: 4 (over z).
Axes of the slice: x: 2, y: 2, z: 4, core: 2. Of those that a mesh axis runs over, the one named last changes fastest.
Arguments:
- tokens: bfloat16 [384, 16, 4096], P('pop'), may hold values from -6 to 6
- weight: bfloat16 [14336, 4096], P('row', 'pop'), may hold values from -0.09375 to 0.09375
- bank_in: bfloat16 [4096, 128], P('row'), may hold values from -0.09375 to 0.09375
- bank_out: bfloat16 [14336, 128], P('row'), may hold values from -6 to 6
- fitness: int32 [384], P('pop'), may hold values from 0 to 191
- past_seeds: int32 [384, 2, 8], P('pop'), may hold values from 0 to 127
- new_seeds: int32 [384, 2, 8], P('pop'), may hold values from 0 to 127
Outputs:
- hidden: bfloat16 [384, 16, 14336], P('pop', None, 'row')
- new_weight: bfloat16 [14336, 4096], P('row', 'pop')
All inputs are finite; a program needn't handle non-finite values.
Results may differ from a plain program's by a relative error of at most 0.012.
Values may be sent and summed in bfloat16 or wider, within the bound.
No kernel may reach another device: no remote copies, remote signals or barrier semaphores. Data moves between devices by JAX's collectives and lax.ppermute only.
A program may use at most 128 MiB of HBM per device.

v0:
```python
import jax
import jax.numpy as jnp
from jax import lax
from jax.sharding import PartitionSpec as P

NOISE_SCALE = 0.1
STEP_SCALE = 0.03


def one_hots(seeds, width):
    levels = jnp.arange(width, dtype=jnp.int32)
    out_hits = (seeds[:, 0, :, None] == levels).astype(jnp.float32)
    in_hits = (seeds[:, 1, :, None] == levels).astype(jnp.float32)
    return (out_hits, in_hits)


def shards(tokens, weight, bank_in, bank_out, fitness, past_seeds, new_seeds):
    members = fitness.shape[0]
    overall = members * lax.axis_size("pop")
    width = bank_out.shape[1]
    everyone = lax.all_gather(fitness, "pop", axis=0, tiled=True)
    lower_count = jnp.sum((everyone[None, :] < fitness[:, None]).astype(jnp.float32), axis=1)
    equal_count = jnp.sum((everyone[None, :] == fitness[:, None]).astype(jnp.float32), axis=1)
    centered = (lower_count + 0.5 * (equal_count - 1.0)) / (overall - 1.0) - 0.5
    out_hits, in_hits = one_hots(past_seeds, width)
    local_coupling = STEP_SCALE * jnp.einsum("m,mki,mkj->ij", centered, out_hits, in_hits)
    coupling = lax.psum(local_coupling, "pop")
    full_in = lax.all_gather(bank_in, "row", axis=0, tiled=True)
    left_part = jnp.dot(bank_out.astype(jnp.float32), coupling, precision=lax.Precision.HIGHEST)
    features = tokens.shape[2]
    flat_tokens = tokens.reshape(members * tokens.shape[1], features)
    own_offset = lax.axis_index("pop") * weight.shape[1]
    columns = lax.dynamic_slice_in_dim(full_in, own_offset, weight.shape[1], 0).astype(jnp.float32)
    update = jnp.dot(left_part, columns.T, precision=lax.Precision.HIGHEST)
    new_weight = (weight.astype(jnp.float32) + update).astype(jnp.bfloat16)
    columns = flat_tokens
    base_part = lax.dot_general(
        columns,
        lax.all_gather(new_weight, "pop", axis=1, tiled=True),
        (((1,), (1,)), ((), ())),
        preferred_element_type=jnp.float32,
    )
    projected = jnp.dot(flat_tokens, full_in, preferred_element_type=jnp.float32).reshape(
        members, tokens.shape[1], width
    )
    hidden_hits, feature_hits = one_hots(new_seeds, width)
    mixing = jnp.einsum("mkb,mkc->mbc", feature_hits, hidden_hits)
    low_term = (NOISE_SCALE * jnp.einsum("mtb,mbc->mtc", projected, mixing)).astype(jnp.bfloat16)
    extra = lax.dot_general(
        low_term.reshape(flat_tokens.shape[0], width),
        bank_out,
        (((1,), (1,)), ((), ())),
        preferred_element_type=jnp.float32,
    )
    hidden = (
        (base_part + extra).astype(jnp.bfloat16).reshape(members, tokens.shape[1], weight.shape[0])
    )
    return (hidden, new_weight)


def solution(mesh):
    placed = (
        P("pop", None, None),
        P("row", "pop"),
        P("row", None),
        P("row", None),
        P("pop"),
        P("pop", None, None),
        P("pop", None, None),
    )
    return jax.shard_map(
        shards,
        mesh=mesh,
        in_specs=placed,
        out_specs=(P("pop", None, "row"), P("row", "pop")),
        check_vma=False,
    )
```

profile of v0, /device:TPU:0, one launch (start us, length us, event | category | flops | bytes accessed | tf_op | source)
XLA Modules:
  0.0 272.2 jit_solution(11762700354457997980)
XLA Ops:
  8.0 0.0 copy-start
  8.0 0.0 all-reduce.3.cloned.1.call-start
  8.1 1.3 dynamic-slice
  10.0 0.9 dynamic-update-slice
  10.9 9.5 %all-reduce = s32[384]{0:T(512)S(1)} all-reduce(s32[384]{0:T(512)S(1)} %dynamic-update-slice), channel_id=1, replica_groups=mesh['pop'=8,'row'=4] {'pop'}, use_global_device_ids=true, to_apply=%add | all-reduce | flops 384 | bytes 3072
  20.4 0.8 convert_reduce_fusion
  21.2 0.7 slice_bitcast_fusion.3
  21.9 0.1 copy.13
  22.0 0.1 copy.14
  22.1 1.0 fusion.16
  23.1 0.0 all-reduce.3.cloned.1.call-update
  23.2 0.0 all-gather.3.cloned.1.call-start
  23.2 0.5 all-gather.3.cloned.1.call-update
  23.7 0.0 all-gather.5.cloned.1.call-start
  23.8 52.4 %all-reduce.3.cloned.1.call-done = f32[128,128]{1,0:T(8,128)} async-done(((f32[128,128]{1,0:T(8,128)}), f32[128,128]{1,0:T(8,128)}) %all-reduce.3.cloned.1.call-update) | async-done | bytes 65552 | tf_op jit(solution)/shard_map/psum | solution.py:27
  76.2 0.0 copy-done
  76.2 1.8 fusion.31
  77.9 0.0 copy-start.1
  77.9 0.0 all-gather.3.cloned.1.call-done
  78.0 6.2 %add_convert_fusion = bf16[3584,512]{1,0:T(8,128)(2,1)} fusion(bf16[3584,512]{1,0:T(8,128)(2,1)} %param.8, f32[128,3584]{1,0:T(8,128)S(1)} %fusion.31, bf16[4096,128]{1,0:T(8,128)(2,1)} %all-gather.3.cloned.1.call-done, s32[]{:T(128)S(6)} %select_n.3), kind=kOutput, calls=%fused_computation.2 | convolution fusion | flops 2824077312 | bytes 9306116 | tf_op jit(solution)/shard_map/dot_general | solution.py:34
  84.2 0.0 all-gather.5.cloned.1.call-update
  84.2 0.0 copy-done.1
  84.2 0.1 copy.15
  84.3 0.1 copy.16
  84.4 6.3 %fusion.11 = bf16[48,16,128]{2,1,0:T(8,128)(2,1)S(1)} fusion(bf16[48,16,4096]{2,1,0:T(8,128)(2,1)} %param.7, bf16[4096,128]{1,0:T(8,128)(2,1)} %all-gather.3.cloned.1.call-done, s32[48,8]{1,0:T(8,128)S(1)} %copy.16, s32[48,8]{1,0:T(8,128)S(1)} %copy.15), kind=kOutput, calls=%fused_computation.7 | convolution fusion | flops 843350016 | bytes 7539712 | tf_op jit(solution)/shard_map/mtb,mbc->mtc/dot_general | solution.py:48
  90.7 141.8 %all-gather.5.cloned.1.call-done = bf16[3584,4096]{1,0:T(8,128)(2,1)} async-done(((bf16[3584,512]{1,0:T(8,128)(2,1)}), bf16[3584,4096]{1,0:T(8,128)(2,1)}) %all-gather.5.cloned.1.call-update) | async-done | bytes 29360144 | tf_op jit(solution)/shard_map/all_gather | solution.py:39
  232.5 28.2 %fusion.32 = f32[3584,768]{0,1:T(8,128)S(1)} fusion(bf16[3584,4096]{1,0:T(8,128)(2,1)} %all-gather.5.cloned.1.call-done, bf16[768,4096]{1,0:T(8,128)(2,1)} %bitcast.34), kind=kOutput, calls=%fused_computation.33 | convolution fusion | flops 22548578304 | bytes 46661632 | tf_op jit(solution)/shard_map/dot_general | solution.py:37
  260.7 4.0 %fusion = bf16[768,3584]{1,0:T(8,128)(2,1)} fusion(f32[3584,768]{0,1:T(8,128)S(1)} %fusion.32, bf16[768,128]{1,0:T(8,128)(2,1)S(1)} %bitcast.33, bf16[3584,128]{1,0:T(8,128)(2,1)S(1)} %copy-done), kind=kOutput, calls=%fused_computation.1 | convolution fusion | flops 710148096 | bytes 17629184 | tf_op jit(solution)/shard_map/dot_general | solution.py:49
  (3 shorter events, 0.0 us)
Async XLA Ops:
  8.0 68.2 %copy-start = (bf16[3584,128]{1,0:T(8,128)(2,1)S(1)}, bf16[3584,128]{1,0:T(8,128)(2,1)}, u32[]{:S(2)}) copy-start(bf16[3584,128]{1,0:T(8,128)(2,1)} %param.10) | copy-start | bytes 2752516
  8.0 68.1 %all-reduce.3.cloned.1.call-start = ((), (), s32[]{:S(2)}) async-start(), calls=%async_computation | async-start | bytes 131072 | tf_op jit(solution)/shard_map/psum | solution.py:27
  23.2 54.8 %all-gather.3.cloned.1.call-start = ((), (), s32[]{:S(2)}) async-start(), calls=%async_computation.1 | async-start | bytes 1310720 | tf_op jit(solution)/shard_map/all_gather | solution.py:28
  23.7 208.8 %all-gather.5.cloned.1.call-start = ((), (), s32[]{:S(2)}) async-start(), calls=%async_computation.2 | async-start | bytes 33030144 | tf_op jit(solution)/shard_map/all_gather | solution.py:39
  77.9 6.3 %copy-start.1 = (s32[48,2,8]{0,2,1:T(8,128)S(1)}, s32[48,2,8]{0,2,1:T(8,128)}, u32[]{:S(2)}) copy-start(s32[48,2,8]{0,2,1:T(8,128)} %param.13) | copy-start | bytes 9220
Sparse Core Ops, SparseCore 0:
  23.3 52.8 all-reduce.2
  84.3 148.1 all-gather.4
Sparse Core Ops, SparseCore 1:
  25.2 27.5 all-gather.2
where the time goes:
time: 272 us
  waiting for transfers between devices  195 us (72%)
  matrix products  47.6 us (18%)
  between operations  16.2 us (6%)
  blocking collectives  9.49 us (3%)
  local copies, waits for them, and re-layouts  3.23 us (1%)
    all_gather x1, waiting for transfers between devices, shards(): lax.all_gather(new_weight, 'pop', axis=1, tiled=True)  142 us
    psum x1, waiting for transfers between devices, shards(): coupling = lax.psum(local_coupling, 'pop')  52.4 us
    dot_general x1, matrix products, shards(): lax.dot_general(columns, lax.all_gather(new_weight, 'pop', axis=1, tiled=...  28.2 us
    unnamed x1, blocking collectives  9.49 us
    dot_general x1, matrix products, shards(): jnp.einsum('mtb,mbc->mtc', projected, mixing)  6.34 us
    dot_general x1, matrix products, shards(): update = jnp.dot(left_part, columns.T, precision=lax.Precision.HIGHEST)  6.22 us
  transfers between devices with their start and end apart: 3, of which 2 were waited for; matrix products, arithmetic and copies ran while one was open for 3% of the time, Pallas kernels for 0%

commit v1 on v0

--- a/solution.py
+++ b/solution.py
@@ -24,7 +24,11 @@
     centered = (lower_count + 0.5 * (equal_count - 1.0)) / (overall - 1.0) - 0.5
     out_hits, in_hits = one_hots(past_seeds, width)
     local_coupling = STEP_SCALE * jnp.einsum("m,mki,mkj->ij", centered, out_hits, in_hits)
-    coupling = lax.psum(local_coupling, "pop")
+
+    def _state_spots(target):
+        return jnp.sum(lax.all_gather(target, "pop"), 0)
+
+    coupling = _state_spots(local_coupling)
     full_in = lax.all_gather(bank_in, "row", axis=0, tiled=True)
     left_part = jnp.dot(bank_out.astype(jnp.float32), coupling, precision=lax.Precision.HIGHEST)
     features = tokens.shape[2]

time: 272 us -> 234 us (0.86)
  waiting for transfers between devices: 195 us -> 150 us
  blocking collectives: 9.49 us -> 18.7 us
    psum x1 -> x0, waiting for transfers between devices: 52.4 us -> none  [shards(): coupling = lax.psum(local_coupling, 'pop')]
    all_gather x0 -> x1, blocking collectives: none -> 9.21 us  [_state_spots(): return jnp.sum(lax.all_gather(target, 'pop'), 0)]
    all_gather x1, waiting for transfers between devices: 0.03 us -> 7.91 us  [shards(): full_in = lax.all_gather(bank_in, 'row', axis=0, tiled=True)]
  transfers between devices with their start and end apart: 3 -> 2, of which waited for: 2 -> 2; matrix products, arithmetic and copies ran while one was open for 3% -> 5% of each run, Pallas kernels for 0% -> 0%
where the time goes in v1:
time: 234 us
  waiting for transfers between devices  150 us (64%)
  matrix products  46.1 us (20%)
  blocking collectives  18.7 us (8%)
  between operations  14.8 us (6%)
  local copies, waits for them, and re-layouts  2.99 us (1%)
    all_gather x1, waiting for transfers between devices, shards(): lax.all_gather(new_weight, 'pop', axis=1, tiled=True)  142 us
    dot_general x1, matrix products, shards(): lax.dot_general(columns, lax.all_gather(new_weight, 'pop', axis=1, tiled=...  28.2 us
    unnamed x1, blocking collectives  9.49 us
    all_gather x1, blocking collectives, _state_spots(): return jnp.sum(lax.all_gather(target, 'pop'), 0)  9.21 us
    all_gather x1, waiting for transfers between devices, shards(): full_in = lax.all_gather(bank_in, 'row', axis=0, tiled=True)  7.91 us
    dot_general x1, matrix products, shards(): jnp.einsum('mtb,mbc->mtc', projected, mixing)  6.35 us
    dot_general x1, matrix products, shards(): update = jnp.dot(left_part, columns.T, precision=lax.Precision.HIGHEST)  6.2 us
  transfers between devices with their start and end apart: 2, of which 2 were waited for; matrix products, arithmetic and copies ran while one was open for 5% of the time, Pallas kernels for 0%

profile of v1, /device:TPU:0, one launch (start us, length us, event | category | flops | bytes accessed | tf_op | source)
XLA Modules:
  0.0 233.9 jit_solution(12375233782503668630)
XLA Ops:
  7.2 0.0 copy-start
  7.2 0.0 all-gather.4.cloned.1.call-start
  7.2 0.7 all-gather.4.cloned.1.call-update
  7.9 0.0 all-gather.6.cloned.1.call-start
  8.0 1.2 dynamic-slice
  9.9 0.9 dynamic-update-slice
  10.7 9.5 %all-reduce = s32[384]{0:T(512)S(1)} all-reduce(s32[384]{0:T(512)S(1)} %dynamic-update-slice), channel_id=1, replica_groups=mesh['pop'=8,'row'=4] {'pop'}, use_global_device_ids=true, to_apply=%add | all-reduce | flops 384 | bytes 3072
  20.2 0.8 convert_reduce_fusion
  21.1 0.7 slice_bitcast_fusion.3
  21.8 0.4 fusion.16
  22.2 9.2 %all-gather = f32[1024,128]{1,0:T(8,128)S(1)} all-gather(f32[128,128]{1,0:T(8,128)S(1)} %fusion.16), channel_id=2, replica_groups=mesh['pop'=8,'row'=4] {'pop'}, dimensions={0}, use_global_device_ids=true | all-gather | bytes 589824 | tf_op jit(solution)/shard_map/all_gather | solution.py:29
  31.4 0.0 copy-done
  31.4 0.9 fusion.31
  32.4 0.0 copy-start.1
  32.4 7.9 %all-gather.4.cloned.1.call-done = bf16[4096,128]{1,0:T(8,128)(2,1)} async-done(((bf16[1024,128]{1,0:T(8,128)(2,1)}), bf16[4096,128]{1,0:T(8,128)(2,1)}) %all-gather.4.cloned.1.call-update) | async-done | bytes 1048592 | tf_op jit(solution)/shard_map/all_gather | solution.py:32
  40.3 6.2 %add_convert_fusion = bf16[3584,512]{1,0:T(8,128)(2,1)} fusion(bf16[3584,512]{1,0:T(8,128)(2,1)} %param.8, f32[128,3584]{1,0:T(8,128)S(1)} %fusion.31, bf16[4096,128]{1,0:T(8,128)(2,1)} %all-gather.4.cloned.1.call-done, s32[]{:T(128)S(6)} %select_n.3), kind=kOutput, calls=%fused_computation.2 | convolution fusion | flops 2824077312 | bytes 9306116 | tf_op jit(solution)/shard_map/dot_general | solution.py:38
  46.5 0.0 all-gather.6.cloned.1.call-update
  46.5 0.0 copy-done.1
  46.5 0.1 copy.11
  46.6 0.1 copy.12
  46.7 6.3 %fusion.11 = bf16[48,16,128]{2,1,0:T(8,128)(2,1)S(1)} fusion(bf16[48,16,4096]{2,1,0:T(8,128)(2,1)} %param.7, bf16[4096,128]{1,0:T(8,128)(2,1)} %all-gather.4.cloned.1.call-done, s32[48,8]{1,0:T(8,128)S(1)} %copy.12, s32[48,8]{1,0:T(8,128)S(1)} %copy.11), kind=kOutput, calls=%fused_computation.7 | convolution fusion | flops 843350016 | bytes 7539712 | tf_op jit(solution)/shard_map/mtb,mbc->mtc/dot_general | solution.py:52
  53.0 141.8 %all-gather.6.cloned.1.call-done = bf16[3584,4096]{1,0:T(8,128)(2,1)} async-done(((bf16[3584,512]{1,0:T(8,128)(2,1)}), bf16[3584,4096]{1,0:T(8,128)(2,1)}) %all-gather.6.cloned.1.call-update) | async-done | bytes 29360144 | tf_op jit(solution)/shard_map/all_gather | solution.py:43
  194.8 28.2 %fusion.32 = f32[3584,768]{0,1:T(8,128)S(1)} fusion(bf16[3584,4096]{1,0:T(8,128)(2,1)} %all-gather.6.cloned.1.call-done, bf16[768,4096]{1,0:T(8,128)(2,1)} %bitcast.36), kind=kOutput, calls=%fused_computation.33 | convolution fusion | flops 22548578304 | bytes 46661632 | tf_op jit(solution)/shard_map/dot_general | solution.py:41
  223.0 4.0 %fusion = bf16[768,3584]{1,0:T(8,128)(2,1)} fusion(f32[3584,768]{0,1:T(8,128)S(1)} %fusion.32, bf16[768,128]{1,0:T(8,128)(2,1)S(1)} %bitcast.35, bf16[3584,128]{1,0:T(8,128)(2,1)S(1)} %copy-done), kind=kOutput, calls=%fused_computation.1 | convolution fusion | flops 710148096 | bytes 17629184 | tf_op jit(solution)/shard_map/dot_general | solution.py:53
  (4 shorter events, 0.0 us)
Async XLA Ops:
  7.2 24.3 %copy-start = (bf16[3584,128]{1,0:T(8,128)(2,1)S(1)}, bf16[3584,128]{1,0:T(8,128)(2,1)}, u32[]{:S(2)}) copy-start(bf16[3584,128]{1,0:T(8,128)(2,1)} %param.10) | copy-start | bytes 2752516
  7.2 33.1 %all-gather.4.cloned.1.call-start = ((), (), s32[]{:S(2)}) async-start(), calls=%async_computation | async-start | bytes 1310720 | tf_op jit(solution)/shard_map/all_gather | solution.py:32
  7.9 186.9 %all-gather.6.cloned.1.call-start = ((), (), s32[]{:S(2)}) async-start(), calls=%async_computation.1 | async-start | bytes 33030144 | tf_op jit(solution)/shard_map/all_gather | solution.py:43
  32.4 14.1 %copy-start.1 = (s32[48,2,8]{0,2,1:T(8,128)S(1)}, s32[48,2,8]{0,2,1:T(8,128)}, u32[]{:S(2)}) copy-start(s32[48,2,8]{0,2,1:T(8,128)} %param.13) | copy-start | bytes 9220
Sparse Core Ops, SparseCore 0:
  9.6 30.6 all-gather.3
  46.6 148.1 all-gather.5
